TPU v7x, 256 devices: a whole 4x4x8 slice. The times are simulated.
256 devices in a mesh: atom: 32 (over x, z_lo, core), chan: 8 (over y, z_hi).
Axes of the slice: x: 4, y: 4, z: 8 (z_hi: 2, z_lo: 4; z = z_hi * 4 + z_lo), core: 2. Of those that a mesh axis runs over, the one named last changes fastest.
Arguments:
- positions: float32 [3, 4096], P(None, 'atom'), may hold values from -9 to 9
- features: bfloat16 [512, 4096], P('chan', 'atom'), may hold values from -6 to 6
- struct_ids: int32 [4096], P('atom'), may hold values from 0 to 31, as said below
- slots: int32 [64, 4096], P(None, 'atom'), may hold values from 0 to 96, as said below
- validity: int32 [64, 4096], P(None, 'atom'), may hold values from 0 to 1, as said below
- radial_in: bfloat16 [512, 128], replicated, may hold values from -72 to 72
- radial_out: bfloat16 [512, 512], P('chan'), may hold values from -0.0234375 to 0.0234375
- mixing: bfloat16 [512, 512], P(None, 'chan'), may hold values from -0.5 to 0.5
- readout: float32 [512], replicated, may hold values from -0.0078125 to 0.0078125
Outputs:
- forces: float32 [3, 4096], P(None, 'atom')
- stress: float32 [9, 32], replicated
Inputs may be any that keep to these rules, and one draw needn't show every extreme that they name: `struct_ids`: structure numbers never fall along the atoms and every structure has at least one atom. `slots`: the 64 slot values of one atom are distinct and never equal 48. `validity`: an edge is valid only where its neighbour atom exists and belongs to the same structure.
All inputs are finite; a program needn't handle non-finite values.
Results may differ from a plain program's by a relative error of at most 0.0099.
Values may be sent and summed in bfloat16 or wider, within the bound.
No kernel may reach another device: no remote copies, remote signals or barrier semaphores. Data moves between devices by JAX's collectives and lax.ppermute only.
A program may use at most 64 MiB of HBM per device.

v0:
```python
import jax
import jax.numpy as jnp
from jax import lax
from jax.sharding import PartitionSpec as P

RIM = 48
sharpness = 40.0
reach = 10.0


def with_halo(value, sides, width):
    for axis, dim in sides:
        size, length = (lax.axis_size(axis), value.shape[dim])
        up = [(i, (i + 1) % size) for i in range(size - 1)]
        down = [(j, i) for i, j in up]
        last = lax.slice_in_dim(value, length - width, length, axis=dim)
        first = lax.slice_in_dim(value, 0, width, axis=dim)
        before = lax.ppermute(last, axis, up)
        after = lax.ppermute(first, axis, down)
        value = jnp.concatenate([before, value, after], axis=dim)
    return value


def turned_gather(arrays, axis, dims):
    turned = [jnp.moveaxis(a, dim, 0) for a, dim in zip(arrays, dims)]
    both = jnp.concatenate([t.reshape(len(t), -1) for t in turned], axis=1)
    result, at, outs = (lax.all_gather(both, axis, axis=0, tiled=True), 0, [])
    for t, dim in zip(turned, dims):
        share = result[:, at : at + t[0].size].reshape(-1, *t.shape[1:])
        outs.append(jnp.moveaxis(share, 0, dim))
        at += t[0].size
    return tuple(outs)


def sent_to_all(value, axis):
    copies = jnp.broadcast_to(value, (lax.axis_size(axis), *value.shape))
    return lax.all_to_all(copies, axis, split_axis=0, concat_axis=0, tiled=True)


def of_everyone(value, axis):
    everything = sent_to_all(value, axis)
    return jnp.sum(everything, axis=0)


def packed_total(arrays, axis):
    flat, at, outs = (jnp.concatenate([a.reshape(-1) for a in arrays]), 0, [])
    running = of_everyone(flat, axis)
    for a in arrays:
        outs.append(running[at : at + a.size].reshape(a.shape))
        at += a.size
    return tuple(outs)


def from_behind(value, axis, by):
    size = lax.axis_size(axis)
    pairs = [(i, i + by) for i in range(size) if 0 <= i + by < size]
    return lax.ppermute(value, axis, pairs)


def dsilu(value):
    sigma = jax.nn.sigmoid(value)
    return sigma * (1.0 + value * (1.0 - sigma))


def radial_terms(vector, radial_in, radial_out):
    dist = jnp.sqrt(1.0 + jnp.sum(vector * vector, axis=0))
    count = radial_in.shape[1]
    centers = jnp.arange(count).astype(jnp.float32) * (reach / count)
    offset = dist[None, :] - centers[:, None]
    bump = jnp.exp(-sharpness * offset * offset)
    basis = bump.astype(jnp.bfloat16)
    slope = (-2.0 * sharpness * offset * bump).astype(jnp.bfloat16)
    pre = jnp.dot(radial_in, basis, preferred_element_type=jnp.float32)
    dpre = jnp.dot(radial_in, slope, preferred_element_type=jnp.float32)
    hidden = jax.nn.silu(pre).astype(jnp.bfloat16)
    dhidden = (dsilu(pre) * dpre).astype(jnp.bfloat16)
    radial = jnp.dot(radial_out, hidden, preferred_element_type=jnp.float32)
    dradial = jnp.dot(radial_out, dhidden, preferred_element_type=jnp.float32)
    return (dist, radial, dradial)


def local(positions, features, struct_ids, slots, validity, radial_in, radial_out, mixing, readout):
    slot_count, atom_count = slots.shape
    padded_feat, padded_pos = (
        with_halo(features.astype(jnp.float32), (("atom", 1),), RIM).astype(features.dtype),
        with_halo(positions, (("atom", 1),), RIM),
    )
    atom_index = jnp.arange(atom_count, dtype=jnp.int32)
    whole_feat, whole_radial, whole_mix = turned_gather(
        (padded_feat, radial_out, mixing), "chan", (0, 0, 1)
    )
    used = slot_count // lax.axis_size("chan")
    first = lax.axis_index("chan") * used
    slot_rows = lax.dynamic_slice_in_dim(slots, first, used, 0)
    valid_rows = lax.dynamic_slice_in_dim(validity, first, used, 0)
    flat_index = (atom_index[None, :] + slot_rows).reshape(-1)
    far_feat = whole_feat[:, flat_index]
    vector = padded_pos[:, flat_index] - jnp.tile(positions, (1, used))
    weight = valid_rows.reshape(-1).astype(jnp.float32)
    dist, radial, dradial = radial_terms(vector, radial_in, whole_radial)
    message = (far_feat * radial).astype(jnp.bfloat16)
    mixed = jnp.dot(whole_mix, message, preferred_element_type=jnp.float32)
    gmix = (weight[None, :] * readout[:, None] * dsilu(mixed)).astype(jnp.bfloat16)
    gmsg = lax.dot_general(
        whole_mix, gmix, (((0,), (0,)), ((), ())), preferred_element_type=jnp.float32
    )
    gdist = jnp.sum(gmsg * far_feat.astype(jnp.float32) * dradial, axis=0)
    gvec = gdist * vector / dist
    outgoing = gvec.reshape(3, used, atom_count).sum(axis=1)
    table = jnp.zeros((3, atom_count + 2 * RIM), jnp.float32).at[:, flat_index].add(-gvec)
    table = table.at[:, RIM : RIM + atom_count].add(outgoing)
    atomvir = (vector[:, None, :] * gvec[None, :, :]).reshape(9, used, atom_count).sum(axis=1)
    table, atomvir = packed_total((table, atomvir), "chan")
    from_next = from_behind(table[:, :RIM], "atom", -1)
    from_prior = from_behind(table[:, RIM + atom_count :], "atom", 1)
    forces = table[:, RIM : RIM + atom_count]
    forces = forces + jnp.pad(from_prior, ((0, 0), (0, atom_count - RIM)))
    forces = forces + jnp.pad(from_next, ((0, 0), (atom_count - RIM, 0)))
    struct_total = atom_count * lax.axis_size("atom") // 128
    onehot = (struct_ids[None, :] == jnp.arange(struct_total, dtype=jnp.int32)[:, None]).astype(
        jnp.float32
    )
    virial = jnp.dot(atomvir, onehot.T, precision=lax.Precision.HIGHEST)
    counts = jnp.sum(onehot, axis=1)
    virial, counts = packed_total((virial, counts), "atom")
    stress = -virial / counts[None, :]
    return (forces, stress)


def solution(mesh):
    placed = (
        P(None, "atom"),
        P("chan", "atom"),
        P("atom"),
        P(None, "atom"),
        P(None, "atom"),
        P(),
        P("chan", None),
        P(None, "chan"),
        P(),
    )
    return jax.shard_map(
        local, mesh=mesh, in_specs=placed, out_specs=(P(None, "atom"), P()), check_vma=False
    )
```

profile of v0, /device:TPU:1, one launch (start us, length us, event | category | flops | bytes accessed | tf_op | source)
XLA Modules:
  0.0 156.5 jit_solution(10200751247860224397)
XLA Ops:
  7.2 0.0 copy-start
  7.2 0.0 all-gather.2.cloned.1.call-start
  7.2 0.9 fusion.56
  8.1 4.9 %collective-permute-start = (bf16[64,48]{1,0:T(8,128)(2,1)S(1)}, bf16[64,48]{1,0:T(8,128)(2,1)S(1)}, u32[]{:S(2)}, u32[]{:S(2)}) collective-permute-start(bf16[64,48]{1,0:T(8,128)(2,1)S(1)} %get-tuple-element.19), channel_id=1, source_target_pairs={{0,8},{8,16},{16,24},{24,32},{32,40},{40,48},{48,56},{56,64},{64,7... | collective-permute-start | bytes 18440 | tf_op jit(solution)/shard_map/ppermute | solution.py:18
  13.0 1.9 %collective-permute-start.1 = (bf16[64,48]{1,0:T(8,128)(2,1)S(1)}, bf16[64,48]{1,0:T(8,128)(2,1)S(1)}, u32[]{:S(2)}, u32[]{:S(2)}) collective-permute-start(bf16[64,48]{1,0:T(8,128)(2,1)S(1)} %get-tuple-element.18), channel_id=1, source_target_pairs={{8,0},{16,8},{24,16},{32,24},{40,32},{48,40},{56,48},{64,56},{72,6... | collective-permute-start | bytes 18440 | tf_op jit(solution)/shard_map/ppermute | solution.py:19
  14.9 0.0 collective-permute-done
  15.0 3.1 %collective-permute-done.1 = bf16[64,48]{1,0:T(8,128)(2,1)S(1)} collective-permute-done((bf16[64,48]{1,0:T(8,128)(2,1)S(1)}, bf16[64,48]{1,0:T(8,128)(2,1)S(1)}, u32[]{:S(2)}, u32[]{:S(2)}) %collective-permute-start.1) | collective-permute-done | bytes 6176 | tf_op jit(solution)/shard_map/ppermute | solution.py:19
  18.1 1.7 %concatenate.17 = bf16[64,1248]{1,0:T(8,128)(2,1)} concatenate(bf16[64,48]{1,0:T(8,128)(2,1)S(1)} %collective-permute-done, bf16[64,128]{1,0:T(8,128)(2,1)} %param.12, bf16[64,48]{1,0:T(8,128)(2,1)S(1)} %collective-permute-done.1, bf16[64,512]{1,0:T(8,128)(2,1)} %param.17, bf16[64,512]{1,0:T(8,128)(2,1)} %bitcast.80), dimensions={1} | concatenate | bytes 319488 | tf_op jit(solution)/shard_map/concatenate | solution.py:26
  19.8 0.0 all-gather.2.cloned.1.call-update
  19.8 0.8 fusion.58
  20.6 1.9 %collective-permute-start.3 = (f32[3,48]{1,0:T(4,128)S(1)}, f32[3,48]{1,0:T(4,128)S(1)}, u32[]{:S(2)}, u32[]{:S(2)}) collective-permute-start(f32[3,48]{1,0:T(4,128)S(1)} %get-tuple-element.25), channel_id=1, source_target_pairs={{8,0},{16,8},{24,16},{32,24},{40,32},{48,40},{56,48},{64,56},{72,6... | collective-permute-start | bytes 1736 | tf_op jit(solution)/shard_map/ppermute | solution.py:19
  22.6 3.6 %collective-permute-start.2 = (f32[3,48]{1,0:T(4,128)S(1)}, f32[3,48]{1,0:T(4,128)S(1)}, u32[]{:S(2)}, u32[]{:S(2)}) collective-permute-start(f32[3,48]{1,0:T(4,128)S(1)} %get-tuple-element.24), channel_id=1, source_target_pairs={{0,8},{8,16},{16,24},{24,32},{32,40},{40,48},{48,56},{56,64},{64,7... | collective-permute-start | bytes 1736 | tf_op jit(solution)/shard_map/ppermute | solution.py:18
  26.2 0.7 dynamic-slice_add_fusion
  26.9 1.3 convert_bitcast_fusion
  28.2 0.7 broadcast_bitcast_fusion
  28.9 0.7 compare_reduce_fusion
  29.6 0.0 collective-permute-done.3
  29.6 0.0 collective-permute-done.2
  29.6 0.8 pad_maximum_fusion.1
  30.4 0.1 copy.79
  30.5 2.8 %gather_fusion.1 = f32[1024,3]{1,0:T(8,128)S(1)} fusion(f32[3,224]{0,1:T(8,128)S(1)} %copy.79, s32[1024]{0:T(1024)S(1)} %broadcast_clamp_fusion), kind=kCustom, calls=%fused_computation.1 | custom fusion | bytes 28672 | tf_op jit(solution)/shard_map/gather | solution.py:98
  33.3 0.2 copy.80
  33.6 0.5 fusion.25
  34.2 52.5 %all-gather.2.cloned.1.call-done = bf16[512,1248]{1,0:T(8,128)(2,1)} async-done(((bf16[64,1248]{1,0:T(8,128)(2,1)}), bf16[512,1248]{1,0:T(8,128)(2,1)}) %all-gather.2.cloned.1.call-update) | async-done | bytes 1277968 | tf_op jit(solution)/shard_map/all_gather | solution.py:27
  86.7 1.0 slice.91
  87.7 0.1 copy.91
  87.8 4.0 %gather_fusion = bf16[1024,512]{1,0:T(8,128)(2,1)S(1)} fusion(bf16[512,224]{0,1:T(8,128)(2,1)S(1)} %copy.91, s32[1024]{0:T(1024)S(1)} %broadcast_clamp_fusion), kind=kCustom, calls=%fused_computation | custom fusion | bytes 2101248 | tf_op jit(solution)/shard_map/gather | solution.py:97
  91.8 0.0 copy-start.3
  91.8 0.0 copy-start.7
  91.8 1.3 copy.78
  93.1 3.6 %multiply_convert_fusion = bf16[512,1024]{0,1:T(8,128)(2,1)S(1)} fusion(bf16[1024,512]{0,1:T(8,128)(2,1)} %copy.78, f32[1024,512]{1,0:T(8,128)S(1)} %fusion.25, f32[512]{0:T(512)S(1)} %copy-done.7, f32[1024]{0:T(1024)S(1)} %copy-done.3, bf16[512,1248]{1,0:T(8,128)(2,1)} %all-gather.2.cloned.1.call-done), kind=kOutput, calls=%fused_computation.19 | convolution fusion | flops 1083179008 | bytes 5249024 | tf_op jit(solution)/shard_map/dot_general | solution.py:102
  96.8 0.0 copy-start.5
  96.8 1.9 %fusion.20 = f32[512,1024]{1,0:T(8,128)S(1)} fusion(bf16[512,1024]{0,1:T(8,128)(2,1)S(1)} %multiply_convert_fusion, bf16[512,1248]{1,0:T(8,128)(2,1)} %all-gather.2.cloned.1.call-done), kind=kOutput, calls=%fused_computation.30 | convolution fusion | flops 536870912 | bytes 3670016 | tf_op jit(solution)/shard_map/dot_general | solution.py:104
  98.7 0.0 copy-start.2
  98.7 0.0 copy-start.6
  98.7 3.5 %fusion.9 = f32[1024]{0:T(1024)S(1)} fusion(f32[512,1024]{1,0:T(8,128)S(1)} %fusion.20, bf16[1024,512]{0,1:T(8,128)(2,1)} %copy.78, f32[1024,512]{1,0:T(8,128)} %copy-done.1, bf16[512,128]{1,0:T(8,128)(2,1)S(1)} %copy-done, bf16[512,1248]{1,0:T(8,128)(2,1)} %all-gather.2.cloned.1.call-done, f32[128]{0:T(128)S(1)} %copy-done.5, f32[1024]{0:T(1024)S(1)} %get-tuple-element.23), kind=kOutput, calls=%fused_computation.18 | convolution fusion | flops 678689792 | bytes 5906944 | tf_op jit(solution)/shard_map/dot_general | solution.py:78
  102.3 0.2 copy.83
  102.5 6.0 %scatter_custom_fusion = f32[3,224]{0,1:T(8,128)S(1)} fusion(s32[1024]{0:T(1024)S(1)} %bitcast.84, f32[1024,3]{1,0:T(8,128)S(1)} %copy.83, f32[]{:T(128)} %constant.45.clone.1), kind=kCustom, calls=%fused_computation.43 | custom fusion | flops 3072 | bytes 2692 | tf_op jit(solution)/shard_map/scatter-add | solution.py:110
  108.6 0.1 copy.84
  108.7 0.7 fusion.38
  109.4 0.1 copy.85
  109.5 0.1 reshape.205
  109.6 0.1 pad_maximum_fusion
  109.7 0.7 broadcast_in_dim.7
  110.3 3.7 %all-to-all-start = ((f32[8,1,1824]{2,1,0:T(1,128)}), f32[8,1,1824]{2,1,0:T(1,128)S(1)}, u32[]{:S(2)}, u32[]{:S(2)}) async-start(f32[8,1,1824]{2,1,0:T(1,128)} %broadcast_in_dim.7), calls=%async_computation | async-start | bytes 122880 | tf_op jit(solution)/shard_map/all_to_all | solution.py:37
  114.1 0.1 convert_reduce_fusion
  114.2 9.0 %all-to-all-done = f32[8,1,1824]{2,1,0:T(1,128)S(1)} async-done(((f32[8,1,1824]{2,1,0:T(1,128)}), f32[8,1,1824]{2,1,0:T(1,128)S(1)}, u32[]{:S(2)}, u32[]{:S(2)}) %all-to-all-start) | async-done | bytes 58400 | tf_op jit(solution)/shard_map/all_to_all | solution.py:37
  123.1 0.1 reduce_sum.67
  123.2 0.2 fusion.41
  123.4 0.1 reshape.207
  123.5 0.1 fusion.57
  123.6 6.9 %collective-permute-start.5 = (f32[3,48]{1,0:T(4,128)S(1)}, f32[3,48]{1,0:T(4,128)S(1)}, u32[]{:S(2)}, u32[]{:S(2)}) collective-permute-start(f32[3,48]{1,0:T(4,128)S(1)} %get-tuple-element.21), channel_id=1, source_target_pairs={{8,0},{16,8},{24,16},{32,24},{40,32},{48,40},{56,48},{64,56},{72,6... | collective-permute-start | bytes 1736 | tf_op jit(solution)/shard_map/ppermute | solution.py:57
  130.4 2.6 %collective-permute-start.4 = (f32[3,48]{1,0:T(4,128)S(1)}, f32[3,48]{1,0:T(4,128)S(1)}, u32[]{:S(2)}, u32[]{:S(2)}) collective-permute-start(f32[3,48]{1,0:T(4,128)S(1)} %get-tuple-element.20), channel_id=1, source_target_pairs={{0,8},{8,16},{16,24},{24,32},{32,40},{40,48},{48,56},{56,64},{64,7... | collective-permute-start | bytes 1736 | tf_op jit(solution)/shard_map/ppermute | solution.py:57
  133.0 0.1 reshape.209
  133.1 0.1 pad_maximum_fusion.2
  133.2 0.6 broadcast_in_dim.8
  133.8 7.3 %all-to-all-start.1 = ((f32[32,1,320]{2,1,0:T(1,128)}), f32[32,1,320]{2,1,0:T(1,128)S(1)}, u32[]{:S(2)}, u32[]{:S(2)}) async-start(f32[32,1,320]{2,1,0:T(1,128)} %broadcast_in_dim.8), calls=%async_computation.1 | async-start | bytes 98304 | tf_op jit(solution)/shard_map/all_to_all | solution.py:37
  141.2 0.0 collective-permute-done.4
  141.2 0.7 fusion.46
  141.9 7.0 %all-to-all-done.1 = f32[32,1,320]{2,1,0:T(1,128)S(1)} async-done(((f32[32,1,320]{2,1,0:T(1,128)}), f32[32,1,320]{2,1,0:T(1,128)S(1)}, u32[]{:S(2)}, u32[]{:S(2)}) %all-to-all-start.1) | async-done | bytes 40992 | tf_op jit(solution)/shard_map/all_to_all | solution.py:37
  148.8 0.1 reduce_sum.69
  148.9 0.1 slice.83
  149.0 0.1 neg.21
  149.1 0.6 broadcast_divide_fusion
  (23 shorter events, 0.2 us)
Async XLA Ops:
  7.2 26.4 %copy-start = (bf16[512,128]{1,0:T(8,128)(2,1)S(1)}, bf16[512,128]{1,0:T(8,128)(2,1)}, u32[]{:S(2)}) copy-start(bf16[512,128]{1,0:T(8,128)(2,1)} %param.16) | copy-start | bytes 393220
  7.2 79.5 %all-gather.2.cloned.1.call-start = ((), (), s32[]{:S(2)}) async-start(), calls=%async_computation.2 | async-start | bytes 1474560 | tf_op jit(solution)/shard_map/all_gather | solution.py:27
  8.1 6.9 %collective-permute-start = (bf16[64,48]{1,0:T(8,128)(2,1)S(1)}, bf16[64,48]{1,0:T(8,128)(2,1)S(1)}, u32[]{:S(2)}, u32[]{:S(2)}) collective-permute-start(bf16[64,48]{1,0:T(8,128)(2,1)S(1)} %get-tuple-element.19), channel_id=1, source_target_pairs={{0,8},{8,16},{16,24},{24,32},{32,40},{40,48},{48,56},{56,64},{64,7... | collective-permute-start | bytes 18440 | tf_op jit(solution)/shard_map/ppermute | solution.py:18
  13.0 5.1 %collective-permute-start.1 = (bf16[64,48]{1,0:T(8,128)(2,1)S(1)}, bf16[64,48]{1,0:T(8,128)(2,1)S(1)}, u32[]{:S(2)}, u32[]{:S(2)}) collective-permute-start(bf16[64,48]{1,0:T(8,128)(2,1)S(1)} %get-tuple-element.18), channel_id=1, source_target_pairs={{8,0},{16,8},{24,16},{32,24},{40,32},{48,40},{56,48},{64,56},{72,6... | collective-permute-start | bytes 18440 | tf_op jit(solution)/shard_map/ppermute | solution.py:19
  20.6 9.0 %collective-permute-start.3 = (f32[3,48]{1,0:T(4,128)S(1)}, f32[3,48]{1,0:T(4,128)S(1)}, u32[]{:S(2)}, u32[]{:S(2)}) collective-permute-start(f32[3,48]{1,0:T(4,128)S(1)} %get-tuple-element.25), channel_id=1, source_target_pairs={{8,0},{16,8},{24,16},{32,24},{40,32},{48,40},{56,48},{64,56},{72,6... | collective-permute-start | bytes 1736 | tf_op jit(solution)/shard_map/ppermute | solution.py:19
  22.6 7.1 %collective-permute-start.2 = (f32[3,48]{1,0:T(4,128)S(1)}, f32[3,48]{1,0:T(4,128)S(1)}, u32[]{:S(2)}, u32[]{:S(2)}) collective-permute-start(f32[3,48]{1,0:T(4,128)S(1)} %get-tuple-element.24), channel_id=1, source_target_pairs={{0,8},{8,16},{16,24},{24,32},{32,40},{40,48},{48,56},{56,64},{64,7... | collective-permute-start | bytes 1736 | tf_op jit(solution)/shard_map/ppermute | solution.py:18
  28.9 5.2 %copy-start.4 = (f32[128]{0:T(128)}, f32[128]{0:T(128)S(1)}, u32[]{:S(2)}) copy-start(f32[128]{0:T(128)S(1)} %convert_multiply_fusion) | copy-start | bytes 1540
  34.1 59.0 %copy-start.1 = (f32[1024,512]{1,0:T(8,128)}, f32[1024,512]{1,0:T(8,128)S(1)}, u32[]{:S(2)}) copy-start(f32[1024,512]{1,0:T(8,128)S(1)} %fusion.25) | copy-start | bytes 6291460
  91.8 1.4 copy-start.3
  91.8 1.4 copy-start.7
  96.8 1.9 %copy-start.5 = (f32[128]{0:T(128)S(1)}, f32[128]{0:T(128)}, u32[]{:S(2)}) copy-start(f32[128]{0:T(128)} %copy-done.4) | copy-start | bytes 1540
  98.7 9.9 %copy-start.2 = (f32[3,128]{1,0:T(4,128)S(1)}, f32[3,128]{1,0:T(4,128)}, u32[]{:S(2)}) copy-start(f32[3,128]{1,0:T(4,128)} %param.11) | copy-start | bytes 4612
  98.7 15.4 %copy-start.6 = (s32[128]{0:T(128)S(1)}, s32[128]{0:T(128)}, u32[]{:S(2)}) copy-start(s32[128]{0:T(128)} %param.13) | copy-start | bytes 1540
  110.3 12.8 %all-to-all-start = ((f32[8,1,1824]{2,1,0:T(1,128)}), f32[8,1,1824]{2,1,0:T(1,128)S(1)}, u32[]{:S(2)}, u32[]{:S(2)}) async-start(f32[8,1,1824]{2,1,0:T(1,128)} %broadcast_in_dim.7), calls=%async_computation | async-start | bytes 122880 | tf_op jit(solution)/shard_map/all_to_all | solution.py:37
  123.6 17.6 %collective-permute-start.5 = (f32[3,48]{1,0:T(4,128)S(1)}, f32[3,48]{1,0:T(4,128)S(1)}, u32[]{:S(2)}, u32[]{:S(2)}) collective-permute-start(f32[3,48]{1,0:T(4,128)S(1)} %get-tuple-element.21), channel_id=1, source_target_pairs={{8,0},{16,8},{24,16},{32,24},{40,32},{48,40},{56,48},{64,56},{72,6... | collective-permute-start | bytes 1736 | tf_op jit(solution)/shard_map/ppermute | solution.py:57
  130.4 10.8 %collective-permute-start.4 = (f32[3,48]{1,0:T(4,128)S(1)}, f32[3,48]{1,0:T(4,128)S(1)}, u32[]{:S(2)}, u32[]{:S(2)}) collective-permute-start(f32[3,48]{1,0:T(4,128)S(1)} %get-tuple-element.20), channel_id=1, source_target_pairs={{0,8},{8,16},{16,24},{24,32},{32,40},{40,48},{48,56},{56,64},{64,7... | collective-permute-start | bytes 1736 | tf_op jit(solution)/shard_map/ppermute | solution.py:57
  133.8 15.0 %all-to-all-start.1 = ((f32[32,1,320]{2,1,0:T(1,128)}), f32[32,1,320]{2,1,0:T(1,128)S(1)}, u32[]{:S(2)}, u32[]{:S(2)}) async-start(f32[32,1,320]{2,1,0:T(1,128)} %broadcast_in_dim.8), calls=%async_computation.1 | async-start | bytes 98304 | tf_op jit(solution)/shard_map/all_to_all | solution.py:37
Sparse Core Ops, SparseCore 0:
  19.9 66.7 all-gather.1
where the time goes:
time: 157 us
  waiting for transfers between devices  71.6 us (46%)
  starting transfers between devices  32.9 us (21%)
  local copies, waits for them, and re-layouts  15.9 us (10%)
  between operations  14.4 us (9%)
  other arithmetic  12 us (8%)
  matrix products  9.72 us (6%)
    all_gather x1, waiting for transfers between devices, turned_gather(): result, at, outs = (lax.all_gather(both, axis, axis=0, tiled=True), 0, [])  52.5 us
    all_to_all x2, waiting for transfers between devices, sent_to_all(): return lax.all_to_all(copies, axis, split_axis=0, concat_axis=0, tiled=True)  16 us
    all_to_all x2, starting transfers between devices, sent_to_all(): return lax.all_to_all(copies, axis, split_axis=0, concat_axis=0, tiled=True)  11.1 us
    ppermute x2, starting transfers between devices, from_behind(): return lax.ppermute(value, axis, pairs)  9.46 us
    ppermute x2, starting transfers between devices, with_halo(): before = lax.ppermute(last, axis, up)  8.56 us
    scatter-add x1, other arithmetic, local(): jnp.zeros((3, atom_count + 2 * RIM), jnp.float32).at[:, flat_index]  6.03 us
    gather x2, local copies, waits for them, and re-layouts, local(): far_feat = whole_feat[:, flat_index]  5.3 us
    ppermute x2, starting transfers between devices, with_halo(): after = lax.ppermute(first, axis, down)  3.83 us
  transfers between devices with their start and end apart: 9, of which 4 were waited for; matrix products, arithmetic and copies ran while one was open for 7% of the time, Pallas kernels for 0%

commit v1 on v0

--- a/solution.py
+++ b/solution.py
@@ -24,7 +24,13 @@
 def turned_gather(arrays, axis, dims):
     turned = [jnp.moveaxis(a, dim, 0) for a, dim in zip(arrays, dims)]
     both = jnp.concatenate([t.reshape(len(t), -1) for t in turned], axis=1)
-    result, at, outs = (lax.all_gather(both, axis, axis=0, tiled=True), 0, [])
+    result, at, outs = (
+        jnp.concatenate(
+            lax.all_to_all(jnp.stack([both] * lax.axis_size(axis)), axis, 0, 0), axis=0
+        ),
+        0,
+        [],
+    )
     for t, dim in zip(turned, dims):
         share = result[:, at : at + t[0].size].reshape(-1, *t.shape[1:])
         outs.append(jnp.moveaxis(share, 0, dim))

time: 157 us -> 128 us (0.82)
  waiting for transfers between devices: 71.6 us -> 39.9 us
  between operations: 14.4 us -> 0.91 us
  starting transfers between devices: 32.9 us -> 44.1 us
  matrix products: 9.72 us -> 13.2 us
  other arithmetic: 12 us -> 15.2 us
  local copies, waits for them, and re-layouts: 15.9 us -> 14.1 us
    all_gather x1 -> x0, waiting for transfers between devices: 52.5 us -> none  [turned_gather(): result, at, outs = (lax.all_gather(both, axis, axis=0, tiled=True), 0, [])]
    ppermute x2, waiting for transfers between devices: 3.12 us -> 24.6 us  [with_halo(): after = lax.ppermute(first, axis, down)]
    all_to_all x0 -> x1, starting transfers between devices: none -> 9.92 us  [turned_gather(): lax.all_to_all(jnp.stack([both] * lax.axis_size(axis)), axis, 0, 0)]
    all_to_all x2, starting transfers between devices: 11.1 us -> 16.3 us  [sent_to_all(): return lax.all_to_all(copies, axis, split_axis=0, concat_axis=0, tiled=True)]
    ppermute x2, starting transfers between devices: 9.46 us -> 5.56 us  [from_behind(): return lax.ppermute(value, axis, pairs)]
  transfers between devices with their start and end apart: 9 -> 9, of which waited for: 4 -> 4; matrix products, arithmetic and copies ran while one was open for 7% -> 9% of each run, Pallas kernels for 0% -> 0%
where the time goes in v1:
time: 128 us; the launch traced here: 127 us
  starting transfers between devices  44.1 us (34%)
  waiting for transfers between devices  39.9 us (31%)
  other arithmetic  15.2 us (12%)
  local copies, waits for them, and re-layouts  14.1 us (11%)
  matrix products  13.2 us (10%)
    ppermute x2, waiting for transfers between devices, with_halo(): after = lax.ppermute(first, axis, down)  24.6 us
    all_to_all x2, starting transfers between devices, sent_to_all(): return lax.all_to_all(copies, axis, split_axis=0, concat_axis=0, tiled=True)  16.3 us
    all_to_all x2, waiting for transfers between devices, sent_to_all(): return lax.all_to_all(copies, axis, split_axis=0, concat_axis=0, tiled=True)  15.3 us
    all_to_all x1, starting transfers between devices, turned_gather(): lax.all_to_all(jnp.stack([both] * lax.axis_size(axis)), axis, 0, 0)  9.92 us
    ppermute x2, starting transfers between devices, with_halo(): before = lax.ppermute(last, axis, up)  8.56 us
    scatter-add x1, other arithmetic, local(): jnp.zeros((3, atom_count + 2 * RIM), jnp.float32).at[:, flat_index]  6.16 us
    ppermute x2, starting transfers between devices, from_behind(): return lax.ppermute(value, axis, pairs)  5.56 us
    dot_general x1, matrix products, local(): mixed = jnp.dot(whole_mix, message, preferred_element_type=jnp.float32)  4.61 us
  transfers between devices with their start and end apart: 9, of which 4 were waited for; matrix products, arithmetic and copies ran while one was open for 9% of the time, Pallas kernels for 0%

profile of v1, /device:TPU:1, one launch (start us, length us, event | category | flops | bytes accessed | tf_op | source)
XLA Modules:
  0.0 127.5 jit_solution(1957305308297885416)
XLA Ops:
  0.6 0.0 copy-start
  0.6 0.9 fusion.56
  1.5 4.9 %collective-permute-start = (bf16[64,48]{1,0:T(8,128)(2,1)S(1)}, bf16[64,48]{1,0:T(8,128)(2,1)S(1)}, u32[]{:S(2)}, u32[]{:S(2)}) collective-permute-start(bf16[64,48]{1,0:T(8,128)(2,1)S(1)} %get-tuple-element.19), channel_id=1, source_target_pairs={{0,8},{8,16},{16,24},{24,32},{32,40},{40,48},{48,56},{56,64},{64,7... | collective-permute-start | bytes 18440 | tf_op jit(solution)/shard_map/ppermute | solution.py:18
  6.4 1.9 %collective-permute-start.1 = (bf16[64,48]{1,0:T(8,128)(2,1)S(1)}, bf16[64,48]{1,0:T(8,128)(2,1)S(1)}, u32[]{:S(2)}, u32[]{:S(2)}) collective-permute-start(bf16[64,48]{1,0:T(8,128)(2,1)S(1)} %get-tuple-element.18), channel_id=1, source_target_pairs={{8,0},{16,8},{24,16},{32,24},{40,32},{48,40},{56,48},{64,56},{72,6... | collective-permute-start | bytes 18440 | tf_op jit(solution)/shard_map/ppermute | solution.py:19
  8.4 0.0 collective-permute-done
  8.4 3.1 %collective-permute-done.1 = bf16[64,48]{1,0:T(8,128)(2,1)S(1)} collective-permute-done((bf16[64,48]{1,0:T(8,128)(2,1)S(1)}, bf16[64,48]{1,0:T(8,128)(2,1)S(1)}, u32[]{:S(2)}, u32[]{:S(2)}) %collective-permute-start.1) | collective-permute-done | bytes 6176 | tf_op jit(solution)/shard_map/ppermute | solution.py:19
  11.5 1.0 concatenate.17
  12.5 0.0 copy-start.2
  12.6 1.1 stack.2
  13.7 9.9 %all-to-all-start = ((bf16[8,64,1248]{2,1,0:T(8,128)(2,1)}), bf16[8,64,1248]{2,1,0:T(8,128)(2,1)S(1)}, u32[]{:S(2)}, u32[]{:S(2)}) async-start(bf16[8,64,1248]{2,1,0:T(8,128)(2,1)} %stack.2), calls=%async_computation | async-start | bytes 2621440 | tf_op jit(solution)/shard_map/all_to_all | solution.py:29
  23.6 0.1 fusion.58
  23.7 1.9 %collective-permute-start.3 = (f32[3,48]{1,0:T(4,128)S(1)}, f32[3,48]{1,0:T(4,128)S(1)}, u32[]{:S(2)}, u32[]{:S(2)}) collective-permute-start(f32[3,48]{1,0:T(4,128)S(1)} %get-tuple-element.25), channel_id=1, source_target_pairs={{8,0},{16,8},{24,16},{32,24},{40,32},{48,40},{56,48},{64,56},{72,6... | collective-permute-start | bytes 1736 | tf_op jit(solution)/shard_map/ppermute | solution.py:19
  25.6 3.6 %collective-permute-start.2 = (f32[3,48]{1,0:T(4,128)S(1)}, f32[3,48]{1,0:T(4,128)S(1)}, u32[]{:S(2)}, u32[]{:S(2)}) collective-permute-start(f32[3,48]{1,0:T(4,128)S(1)} %get-tuple-element.24), channel_id=1, source_target_pairs={{0,8},{8,16},{16,24},{24,32},{32,40},{40,48},{48,56},{56,64},{64,7... | collective-permute-start | bytes 1736 | tf_op jit(solution)/shard_map/ppermute | solution.py:18
  29.3 0.7 dynamic-slice_add_fusion
  30.0 1.3 %convert_bitcast_fusion = f32[1024]{0:T(1024)} fusion(s32[64,128]{1,0:T(8,128)} %param.15, s32[]{:T(128)S(6)} %select_n.16), kind=kLoop, calls=%fused_computation.65 | loop fusion | flops 1024 | bytes 8196 | tf_op jit(solution)/shard_map/convert_element_type | solution.py:105
  31.3 0.0 copy-start.5
  31.3 0.6 compare_reduce_fusion
  31.9 21.5 %collective-permute-done.3 = f32[3,48]{1,0:T(4,128)S(1)} collective-permute-done((f32[3,48]{1,0:T(4,128)S(1)}, f32[3,48]{1,0:T(4,128)S(1)}, u32[]{:S(2)}, u32[]{:S(2)}) %collective-permute-start.3) | collective-permute-done | bytes 608 | tf_op jit(solution)/shard_map/ppermute | solution.py:19
  53.4 0.0 collective-permute-done.2
  53.4 0.1 pad_maximum_fusion.1
  53.5 0.1 copy.73
  53.6 2.8 %gather_fusion.1 = f32[1024,3]{1,0:T(8,128)S(1)} fusion(f32[3,224]{0,1:T(8,128)S(1)} %copy.73, s32[1024]{0:T(1024)S(1)} %broadcast_clamp_fusion), kind=kCustom, calls=%fused_computation.1 | custom fusion | bytes 28672 | tf_op jit(solution)/shard_map/gather | solution.py:104
  56.4 0.2 copy.74
  56.6 0.6 multiply_reduce_fusion
  57.2 0.6 fusion.55
  57.8 1.9 %fusion.25 = f32[1024,512]{1,0:T(8,128)} fusion(bf16[512,128]{1,0:T(8,128)(2,1)S(1)} %copy-done, f32[128]{0:T(128)S(1)} %convert_multiply_fusion, f32[1024]{0:T(1024)S(1)} %get-tuple-element.23), kind=kOutput, calls=%fused_computation.33 | convolution fusion | flops 134742016 | bytes 2232832 | tf_op jit(solution)/shard_map/dot_general | solution.py:79
  59.7 0.0 all-to-all-done
  59.8 0.1 copy.85
  59.9 4.0 %gather_fusion = bf16[1024,512]{1,0:T(8,128)(2,1)S(1)} fusion(bf16[512,224]{0,1:T(8,128)(2,1)S(1)} %copy.85, s32[1024]{0:T(1024)S(1)} %broadcast_clamp_fusion), kind=kCustom, calls=%fused_computation | custom fusion | bytes 2101248 | tf_op jit(solution)/shard_map/gather | solution.py:103
  63.9 0.5 copy.72
  64.4 1.0 copy-done.1
  65.4 4.6 %multiply_convert_fusion = bf16[512,1024]{0,1:T(8,128)(2,1)} fusion(bf16[1024,512]{0,1:T(8,128)(2,1)S(1)} %copy.72, f32[1024,512]{1,0:T(8,128)} %fusion.25, f32[512]{0:T(512)} %param.19, f32[1024]{0:T(1024)} %convert_bitcast_fusion, bf16[512,1248]{1,0:T(8,128)(2,1)S(1)} %bitcast.81), kind=kOutput, calls=%fused_computation.19 | convolution fusion | flops 1083179008 | bytes 5249024 | tf_op jit(solution)/shard_map/dot_general | solution.py:108
  70.0 2.0 %fusion.20 = f32[512,1024]{1,0:T(8,128)S(1)} fusion(bf16[512,1024]{0,1:T(8,128)(2,1)} %multiply_convert_fusion, bf16[512,1248]{1,0:T(8,128)(2,1)S(1)} %bitcast.82), kind=kOutput, calls=%fused_computation.30 | convolution fusion | flops 536870912 | bytes 3670016 | tf_op jit(solution)/shard_map/dot_general | solution.py:110
  72.0 3.9 %fusion.9 = f32[1024]{0:T(1024)} fusion(f32[512,1024]{1,0:T(8,128)S(1)} %fusion.20, bf16[1024,512]{0,1:T(8,128)(2,1)} %copy-done.1, f32[1024,512]{1,0:T(8,128)} %fusion.25, bf16[512,128]{1,0:T(8,128)(2,1)S(1)} %copy-done, bf16[512,1248]{1,0:T(8,128)(2,1)S(1)} %bitcast.83, f32[128]{0:T(128)} %copy-done.5, f32[1024]{0:T(1024)} %copy-done.3), kind=kOutput, calls=%fused_computation.18 | convolution fusion | flops 678689792 | bytes 5906944 | tf_op jit(solution)/shard_map/dot_general | solution.py:84
  75.9 0.7 negate_bitcast_fusion
  76.7 0.7 broadcast_multiply_fusion
  77.4 0.2 copy.77
  77.7 6.2 %scatter_custom_fusion = f32[3,224]{0,1:T(8,128)S(1)} fusion(s32[1024]{0:T(1024)} %bitcast.89, f32[1024,3]{1,0:T(8,128)S(1)} %copy.77, f32[]{:T(128)} %constant.45.clone.1), kind=kCustom, calls=%fused_computation.43 | custom fusion | flops 3072 | bytes 3200 | tf_op jit(solution)/shard_map/scatter-add | solution.py:116
  83.8 0.7 fusion.44
  84.6 0.1 copy.78
  84.7 0.6 fusion.38
  85.3 0.1 copy.79
  85.3 0.1 reshape.211
  85.4 0.1 pad_maximum_fusion
  85.5 0.7 broadcast_in_dim.7
  86.2 9.3 %all-to-all-start.1 = ((f32[8,1,1824]{2,1,0:T(1,128)}), f32[8,1,1824]{2,1,0:T(1,128)S(1)}, u32[]{:S(2)}, u32[]{:S(2)}) async-start(f32[8,1,1824]{2,1,0:T(1,128)} %broadcast_in_dim.7), calls=%async_computation.1 | async-start | bytes 122880 | tf_op jit(solution)/shard_map/all_to_all | solution.py:43
  95.5 0.8 convert_reduce_fusion
  96.2 8.3 %all-to-all-done.1 = f32[8,1,1824]{2,1,0:T(1,128)S(1)} async-done(((f32[8,1,1824]{2,1,0:T(1,128)}), f32[8,1,1824]{2,1,0:T(1,128)S(1)}, u32[]{:S(2)}, u32[]{:S(2)}) %all-to-all-start.1) | async-done | bytes 58400 | tf_op jit(solution)/shard_map/all_to_all | solution.py:43
  104.5 0.1 reduce_sum.67
  104.6 0.8 fusion.41
  105.4 0.1 reshape.213
  105.5 0.1 fusion.57
  105.6 1.9 %collective-permute-start.5 = (f32[3,48]{1,0:T(4,128)S(1)}, f32[3,48]{1,0:T(4,128)S(1)}, u32[]{:S(2)}, u32[]{:S(2)}) collective-permute-start(f32[3,48]{1,0:T(4,128)S(1)} %get-tuple-element.21), channel_id=1, source_target_pairs={{8,0},{16,8},{24,16},{32,24},{40,32},{48,40},{56,48},{64,56},{72,6... | collective-permute-start | bytes 1736 | tf_op jit(solution)/shard_map/ppermute | solution.py:63
  107.5 3.6 %collective-permute-start.4 = (f32[3,48]{1,0:T(4,128)S(1)}, f32[3,48]{1,0:T(4,128)S(1)}, u32[]{:S(2)}, u32[]{:S(2)}) collective-permute-start(f32[3,48]{1,0:T(4,128)S(1)} %get-tuple-element.20), channel_id=1, source_target_pairs={{0,8},{8,16},{16,24},{24,32},{32,40},{40,48},{48,56},{56,64},{64,7... | collective-permute-start | bytes 1736 | tf_op jit(solution)/shard_map/ppermute | solution.py:63
  111.2 0.1 reshape.215
  111.3 0.1 pad_maximum_fusion.2
  111.3 0.6 broadcast_in_dim.8
  112.0 7.0 %all-to-all-start.2 = ((f32[32,1,320]{2,1,0:T(1,128)}), f32[32,1,320]{2,1,0:T(1,128)S(1)}, u32[]{:S(2)}, u32[]{:S(2)}) async-start(f32[32,1,320]{2,1,0:T(1,128)} %broadcast_in_dim.8), calls=%async_computation.2 | async-start | bytes 98304 | tf_op jit(solution)/shard_map/all_to_all | solution.py:43
  119.0 0.7 fusion.46
  119.7 7.0 %all-to-all-done.2 = f32[32,1,320]{2,1,0:T(1,128)S(1)} async-done(((f32[32,1,320]{2,1,0:T(1,128)}), f32[32,1,320]{2,1,0:T(1,128)S(1)}, u32[]{:S(2)}, u32[]{:S(2)}) %all-to-all-start.2) | async-done | bytes 40992 | tf_op jit(solution)/shard_map/all_to_all | solution.py:43
  126.6 0.1 reduce_sum.69
  126.7 0.1 slice.83
  126.8 0.1 neg.21
  126.9 0.6 broadcast_divide_fusion
  (19 shorter events, 0.1 us)
Async XLA Ops:
  0.6 57.2 %copy-start = (bf16[512,128]{1,0:T(8,128)(2,1)S(1)}, bf16[512,128]{1,0:T(8,128)(2,1)}, u32[]{:S(2)}) copy-start(bf16[512,128]{1,0:T(8,128)(2,1)} %param.16) | copy-start | bytes 393220
  1.5 6.9 %collective-permute-start = (bf16[64,48]{1,0:T(8,128)(2,1)S(1)}, bf16[64,48]{1,0:T(8,128)(2,1)S(1)}, u32[]{:S(2)}, u32[]{:S(2)}) collective-permute-start(bf16[64,48]{1,0:T(8,128)(2,1)S(1)} %get-tuple-element.19), channel_id=1, source_target_pairs={{0,8},{8,16},{16,24},{24,32},{32,40},{40,48},{48,56},{56,64},{64,7... | collective-permute-start | bytes 18440 | tf_op jit(solution)/shard_map/ppermute | solution.py:18
  6.4 5.1 %collective-permute-start.1 = (bf16[64,48]{1,0:T(8,128)(2,1)S(1)}, bf16[64,48]{1,0:T(8,128)(2,1)S(1)}, u32[]{:S(2)}, u32[]{:S(2)}) collective-permute-start(bf16[64,48]{1,0:T(8,128)(2,1)S(1)} %get-tuple-element.18), channel_id=1, source_target_pairs={{8,0},{16,8},{24,16},{32,24},{40,32},{48,40},{56,48},{64,56},{72,6... | collective-permute-start | bytes 18440 | tf_op jit(solution)/shard_map/ppermute | solution.py:19
  12.5 11.1 %copy-start.2 = (f32[3,128]{1,0:T(4,128)S(1)}, f32[3,128]{1,0:T(4,128)}, u32[]{:S(2)}) copy-start(f32[3,128]{1,0:T(4,128)} %param.11) | copy-start | bytes 4612
  13.7 46.0 %all-to-all-start = ((bf16[8,64,1248]{2,1,0:T(8,128)(2,1)}), bf16[8,64,1248]{2,1,0:T(8,128)(2,1)S(1)}, u32[]{:S(2)}, u32[]{:S(2)}) async-start(bf16[8,64,1248]{2,1,0:T(8,128)(2,1)} %stack.2), calls=%async_computation | async-start | bytes 2621440 | tf_op jit(solution)/shard_map/all_to_all | solution.py:29
  23.7 29.7 %collective-permute-start.3 = (f32[3,48]{1,0:T(4,128)S(1)}, f32[3,48]{1,0:T(4,128)S(1)}, u32[]{:S(2)}, u32[]{:S(2)}) collective-permute-start(f32[3,48]{1,0:T(4,128)S(1)} %get-tuple-element.25), channel_id=1, source_target_pairs={{8,0},{16,8},{24,16},{32,24},{40,32},{48,40},{56,48},{64,56},{72,6... | collective-permute-start | bytes 1736 | tf_op jit(solution)/shard_map/ppermute | solution.py:19
  25.6 27.8 %collective-permute-start.2 = (f32[3,48]{1,0:T(4,128)S(1)}, f32[3,48]{1,0:T(4,128)S(1)}, u32[]{:S(2)}, u32[]{:S(2)}) collective-permute-start(f32[3,48]{1,0:T(4,128)S(1)} %get-tuple-element.24), channel_id=1, source_target_pairs={{0,8},{8,16},{16,24},{24,32},{32,40},{40,48},{48,56},{56,64},{64,7... | collective-permute-start | bytes 1736 | tf_op jit(solution)/shard_map/ppermute | solution.py:18
  31.2 22.2 %copy-start.4 = (s32[1024,1]{0,1:T(1,128)}, s32[1024,1]{0,1:T(1,128)S(1)}, u32[]{:S(2)}) copy-start(s32[1024,1]{0,1:T(1,128)S(1)} %compare_select_fusion) | copy-start | bytes 12292
  31.3 28.5 %copy-start.5 = (f32[128]{0:T(128)}, f32[128]{0:T(128)S(1)}, u32[]{:S(2)}) copy-start(f32[128]{0:T(128)S(1)} %convert_multiply_fusion) | copy-start | bytes 1540
  57.8 1.9 %copy-start.3 = (f32[1024]{0:T(1024)}, f32[1024]{0:T(1024)S(1)}, u32[]{:S(2)}) copy-start(f32[1024]{0:T(1024)S(1)} %get-tuple-element.23) | copy-start | bytes 12292
  64.4 1.0 copy-start.1
  86.2 18.4 %all-to-all-start.1 = ((f32[8,1,1824]{2,1,0:T(1,128)}), f32[8,1,1824]{2,1,0:T(1,128)S(1)}, u32[]{:S(2)}, u32[]{:S(2)}) async-start(f32[8,1,1824]{2,1,0:T(1,128)} %broadcast_in_dim.7), calls=%async_computation.1 | async-start | bytes 122880 | tf_op jit(solution)/shard_map/all_to_all | solution.py:43
  105.6 13.4 %collective-permute-start.5 = (f32[3,48]{1,0:T(4,128)S(1)}, f32[3,48]{1,0:T(4,128)S(1)}, u32[]{:S(2)}, u32[]{:S(2)}) collective-permute-start(f32[3,48]{1,0:T(4,128)S(1)} %get-tuple-element.21), channel_id=1, source_target_pairs={{8,0},{16,8},{24,16},{32,24},{40,32},{48,40},{56,48},{64,56},{72,6... | collective-permute-start | bytes 1736 | tf_op jit(solution)/shard_map/ppermute | solution.py:63
  107.5 11.5 %collective-permute-start.4 = (f32[3,48]{1,0:T(4,128)S(1)}, f32[3,48]{1,0:T(4,128)S(1)}, u32[]{:S(2)}, u32[]{:S(2)}) collective-permute-start(f32[3,48]{1,0:T(4,128)S(1)} %get-tuple-element.20), channel_id=1, source_target_pairs={{0,8},{8,16},{16,24},{24,32},{32,40},{40,48},{48,56},{56,64},{64,7... | collective-permute-start | bytes 1736 | tf_op jit(solution)/shard_map/ppermute | solution.py:63
  112.0 14.6 %all-to-all-start.2 = ((f32[32,1,320]{2,1,0:T(1,128)}), f32[32,1,320]{2,1,0:T(1,128)S(1)}, u32[]{:S(2)}, u32[]{:S(2)}) async-start(f32[32,1,320]{2,1,0:T(1,128)} %broadcast_in_dim.8), calls=%async_computation.2 | async-start | bytes 98304 | tf_op jit(solution)/shard_map/all_to_all | solution.py:43
